TPU v7x, 32 devices: a whole 2x2x4 slice. The times are simulated.
32 devices in a mesh: rep: 8 (over y, x, core), tp: 4 (over z).
Axes of the slice: x: 2, y: 2, z: 4, core: 2. Of those that a mesh axis runs over, the one named last changes fastest.
Arguments:
- tokens: bfloat16 [4096, 8192], P('rep'), may hold values from -6 to 6
- query_weight: float32 [8192, 8192], P(('rep', 'tp')), may hold values from -0.0625 to 0.0625
- key_weight: float32 [8192, 1024], P(('rep', 'tp')), may hold values from -0.0625 to 0.0625
- value_weight: float32 [8192, 1024], P(('rep', 'tp')), may hold values from -0.0625 to 0.0625
- cache_keys: bfloat16 [256, 128, 1024], P('rep', None, 'tp'), may hold values from -240 to 240
- cache_values: bfloat16 [256, 128, 1024], P('rep', None, 'tp'), may hold values from -6 to 6
- lengths: int32 [8, 2], P('rep'), may hold values from 1 to 2048
- page_table: int32 [8, 2, 16], P('rep'), may hold values from 0 to 31, as said below
Outputs:
- attended: bfloat16 [4096, 8192], P('rep', 'tp')
- new_cache: bfloat16 [2, 4096, 1024], P(None, 'rep', 'tp')
Inputs may be any that keep to these rules, and one draw needn't show every extreme that they name: For each group g, the 2 x 16 entries of page_table[g] name each of the group's local pool pages 0 to 31 exactly once.
All inputs are finite; a program needn't handle non-finite values.
Results may differ from a plain program's by a relative error of at most 0.008.
The roundings to bfloat16 on the way count: a program that leaves them out, or rounds other values in their place, can miss the bound.
Values may be sent and summed in bfloat16 or wider, within the bound.
A program may use at most 192 MiB of HBM per device.

v0:
```python
import jax
import jax.numpy as jnp
from jax import lax
from jax.sharding import PartitionSpec as P

HEADS = 64
KV_HEADS = 8
HEAD_DIM = 128
SEQS = 2
NEW = 256
TOK = 512
MAXLEN = 2048


ROPE_THETA = 500000.0


def rotate(vectors, positions):
    half_dim = HEAD_DIM // 2
    frequency = ROPE_THETA ** (-2.0 * jnp.arange(half_dim, dtype=jnp.float32) / HEAD_DIM)
    angles = positions.astype(jnp.float32)[:, None] * frequency[None, :]
    cosine_part = jnp.cos(angles)[:, None, :]
    sine_part = jnp.sin(angles)[:, None, :]
    first_half = vectors[..., :half_dim]
    second_half = vectors[..., half_dim:]
    return jnp.concatenate(
        [
            first_half * cosine_part - second_half * sine_part,
            second_half * cosine_part + first_half * sine_part,
        ],
        axis=-1,
    )


def per_device(
    tokens, query_weight, key_weight, value_weight, cache_keys, cache_values, lengths, page_table
):
    weights = (
        query_weight.astype(jnp.bfloat16),
        key_weight.astype(jnp.bfloat16),
        value_weight.astype(jnp.bfloat16),
    )
    slabs = (
        lax.all_to_all(weights[0], "tp", split_axis=1, concat_axis=0, tiled=True),
        lax.all_to_all(weights[1], "tp", split_axis=1, concat_axis=0, tiled=True),
        lax.all_to_all(weights[2], "tp", split_axis=1, concat_axis=0, tiled=True),
    )
    pieces = (
        lax.all_gather(slabs[0], "rep", axis=0, tiled=True),
        lax.all_gather(slabs[1], "rep", axis=0, tiled=True),
        lax.all_gather(slabs[2], "rep", axis=0, tiled=True),
    )
    raw_query, raw_key, raw_value = tuple(
        (jnp.dot(tokens, piece, preferred_element_type=jnp.float32) for piece in pieces)
    )
    kv_local = raw_key.shape[1] // HEAD_DIM
    group_size = HEADS // KV_HEADS
    scale = 1.0 / HEAD_DIM**0.5
    seq_lengths = lengths[0]
    positions = (seq_lengths[:, None] + jnp.arange(NEW, dtype=jnp.int32)[None, :]).reshape(TOK)
    queries = rotate(raw_query.reshape(TOK, kv_local * group_size, HEAD_DIM), positions).astype(
        jnp.bfloat16
    )
    new_keys = rotate(raw_key.reshape(TOK, kv_local, HEAD_DIM), positions).astype(jnp.bfloat16)
    new_values = raw_value.astype(jnp.bfloat16).reshape(TOK, kv_local, HEAD_DIM)

    def one_sequence(inner):
        seq_queries, seq_keys, seq_values, page_rows, length = inner
        old_keys = cache_keys[page_rows].reshape(MAXLEN, kv_local, HEAD_DIM)
        old_values = cache_values[page_rows].reshape(MAXLEN, kv_local, HEAD_DIM)
        all_keys = jnp.concatenate([old_keys, seq_keys], axis=0)
        all_values = jnp.concatenate([old_values, seq_values], axis=0)
        grouped = seq_queries.reshape(NEW, kv_local, group_size, HEAD_DIM)
        scores = (
            jnp.einsum("nkgd,mkd->kgnm", grouped, all_keys, preferred_element_type=jnp.float32)
            * scale
        )
        key_index = jnp.arange(MAXLEN + NEW, dtype=jnp.int32)[None, :]
        query_index = jnp.arange(NEW, dtype=jnp.int32)[:, None]
        visible = jnp.where(
            key_index < MAXLEN, key_index < length, key_index - MAXLEN <= query_index
        )
        scores = jnp.where(visible[None, None], scores, -1e30)
        maxima = jnp.max(scores, axis=-1, keepdims=True)
        expons = jnp.exp(scores - maxima)
        probs = (expons / jnp.sum(expons, axis=-1, keepdims=True)).astype(jnp.bfloat16)
        output = jnp.einsum("kgnm,mkd->nkgd", probs, all_values, preferred_element_type=jnp.float32)
        return output.astype(jnp.bfloat16).reshape(NEW, kv_local * group_size * HEAD_DIM)

    attended = lax.map(
        one_sequence,
        (
            queries.reshape(SEQS, NEW, kv_local * group_size, HEAD_DIM),
            new_keys.reshape(SEQS, NEW, kv_local, HEAD_DIM),
            new_values.reshape(SEQS, NEW, kv_local, HEAD_DIM),
            page_table[0],
            seq_lengths,
        ),
    )
    new_cache = jnp.stack(
        [new_keys.reshape(TOK, kv_local * HEAD_DIM), new_values.reshape(TOK, kv_local * HEAD_DIM)]
    )
    return (attended.reshape(TOK, kv_local * group_size * HEAD_DIM), new_cache)


def solution(mesh):
    return jax.shard_map(
        per_device,
        mesh=mesh,
        in_specs=(
            P("rep", None),
            P(("rep", "tp"), None),
            P(("rep", "tp"), None),
            P(("rep", "tp"), None),
            P("rep", None, "tp"),
            P("rep", None, "tp"),
            P("rep", None),
            P("rep", None, None),
        ),
        out_specs=(P("rep", "tp"), P(None, "rep", "tp")),
        check_vma=False,
    )
```

profile of v0, /device:TPU:0, one launch (start us, length us, event | category | flops | bytes accessed | tf_op | source)
XLA Modules:
  0.0 450.6 jit_solution(10481622972108164320)
XLA Ops:
  7.2 1.5 copy.33
  8.7 20.6 %all_to_all.57 = bf16[256,4,256]{0,2,1:T(8,128)(2,1)S(1)} all-to-all(bf16[256,4,256]{0,2,1:T(8,128)(2,1)S(1)} %bitcast.110), channel_id=1, replica_groups=mesh['rep'=8,'tp'=4] {'tp'}, dimensions={1} | all-to-all | bytes 1048576 | tf_op jit(solution)/shard_map/all_to_all | solution.py:45
  29.4 1.0 copy.34
  30.7 16.6 %all_to_all.58 = bf16[256,4,256]{0,2,1:T(8,128)(2,1)S(1)} all-to-all(bf16[256,4,256]{0,2,1:T(8,128)(2,1)S(1)} %bitcast.111), channel_id=1, replica_groups=mesh['rep'=8,'tp'=4] {'tp'}, dimensions={1} | all-to-all | bytes 1048576 | tf_op jit(solution)/shard_map/all_to_all | solution.py:46
  47.3 1.0 copy.32
  48.3 7.6 %copy.35 = bf16[256,8192]{0,1:T(8,128)(2,1)} copy(f32[256,8192]{1,0:T(8,128)} %param.11) | data formatting | bytes 12582912 | tf_op args[1]
  55.9 97.8 %all_to_all.59 = bf16[256,4,2048]{0,2,1:T(8,128)(2,1)} all-to-all(bf16[256,4,2048]{0,2,1:T(8,128)(2,1)} %bitcast.105), channel_id=1, replica_groups=mesh['rep'=8,'tp'=4] {'tp'}, dimensions={1} | all-to-all | bytes 8388608 | tf_op jit(solution)/shard_map/all_to_all | solution.py:44
  153.8 6.3 %copy.36 = bf16[4,256,2048]{2,1,0:T(8,128)(2,1)} copy(bf16[4,256,2048]{1,2,0:T(8,128)(2,1)} %bitcast.107) | data formatting | bytes 8388608 | tf_op jit(solution)/shard_map/all_to_all | solution.py:44
  161.4 7.1 %fusion.23 = f32[512,256]{0,1:T(8,128)S(1)} fusion(bf16[512,8192]{1,0:T(8,128)(2,1)} %param.10, bf16[8192,256]{1,0:T(8,128)(2,1)} %all-gather.6.cloned.1.call-done), kind=kOutput, calls=%fused_computation.51 | convolution fusion | flops 2147483648 | bytes 13107200 | tf_op jit(solution)/shard_map/dot_general | solution.py:54
  169.2 9.0 %convolution_convert_fusion = bf16[512,256]{1,0:T(8,128)(2,1)S(1)} fusion(bf16[512,8192]{1,0:T(8,128)(2,1)} %param.10, bf16[8192,256]{1,0:T(8,128)(2,1)} %all-gather.4.cloned.1.call-done), kind=kOutput, calls=%fused_computation.40 | convolution fusion | flops 2147614720 | bytes 12845056 | tf_op jit(solution)/shard_map/dot_general | solution.py:54
  179.2 0.8 pad_maximum_fusion.1
  180.0 140.0 %all-gather.8.cloned.1.call-done = bf16[8192,2048]{1,0:T(8,128)(2,1)} async-done(((bf16[1024,2048]{1,0:T(8,128)(2,1)}), bf16[8192,2048]{1,0:T(8,128)(2,1)}) %all-gather.8.cloned.1.call-update) | async-done | bytes 33554448 | tf_op jit(solution)/shard_map/all_gather | solution.py:49
  320.0 25.8 %fusion.24 = f32[512,2048]{0,1:T(8,128)} fusion(bf16[512,8192]{1,0:T(8,128)(2,1)} %param.10, bf16[8192,2048]{1,0:T(8,128)(2,1)} %all-gather.8.cloned.1.call-done), kind=kOutput, calls=%fused_computation.52 | convolution fusion | flops 17179869184 | bytes 46137344 | tf_op jit(solution)/shard_map/reshape | solution.py:61
  345.8 2.9 subtract_convert_fusion
  349.0 1.1 concatenate.37
  350.2 3.9 pad_maximum_fusion
  354.1 3.7 copy.41
  357.8 86.2 %while.12 = (s32[]{:T(128)}, bf16[2,256,2048]{2,1,0:T(8,128)(2,1)}, s32[2,16]{1,0:T(2,128)S(1)}, bf16[32,128,256]{2,1,0:T(8,128)(2,1)}, bf16[2,256,2,128]{3,2,1,...) while((s32[]{:T(128)}, bf16[2,256,2048]{2,1,0:T(8,128)(2,1)}, ...), condition=%wide.region_3.4_spmd, body=%wide.region_0.3_spmd.sunk | while | flops 4894894080 | bytes 100859848 | solution.py:90
  359.1 1.9 fusion.39
  361.0 2.2 gather_fusion
  363.7 1.3 constant_dynamic-slice_fusion.5
  365.0 17.5 %fusion.41 = (f32[2,8,256]{2,1,0:T(8,128)S(1)}, f32[2,8,256,2304]{2,3,1,0:T(8,128)}) fusion(bf16[256,2,8,128]{3,0,2,1:T(8,128)(2,1)S(1)} %bitcast.103, pred[256,2304]{0,1:T(8,128)(4,1)S(1)} %fusion.39, bf16[256,2,128]{2,0,1:T(8,128)(2,1)S(1)} %dynamic-slice_bitcast_fusion.2, bf16[2048,2,128]{2,0,1:T(8,128)(2,1)S(1)} %copy.60), kind=kOutput, calls=%fused_computation.50.clone.1 | convolution fusion | flops 2456029440 | bytes 40583168 | tf_op jit(solution)/shard_map/while/body/eval_jaxpr/sub | solution.py:85
  382.4 2.2 gather_fusion.1
  386.0 13.3 %fusion.42 = bf16[2,128,8,256]{3,1,2,0:T(8,128)(2,1)S(1)} fusion(f32[2,8,256,2304]{2,3,1,0:T(8,128)} %get-tuple-element.232, f32[2,8,256]{2,1,0:T(8,128)S(1)} %get-tuple-element.233, bf16[256,2,128]{0,2,1:T(8,128)(2,1)S(1)} %bitcast.109, bf16[2048,2,128]{0,2,1:T(8,128)(2,1)S(1)} %copy.62), kind=kOutput, calls=%fused_computation.14.clone.1 | convolution fusion | flops 2437677056 | bytes 39993344 | tf_op jit(solution)/shard_map/while/body/eval_jaxpr/kgnm,mkd->nkgd/dot_general | solution.py:87
  399.9 1.0 constant_dynamic-update-slice_fusion.2
  402.2 1.9 fusion.39
  404.1 2.2 gather_fusion
  406.8 1.3 constant_dynamic-slice_fusion.5
  408.1 17.5 %fusion.41 = (f32[2,8,256]{2,1,0:T(8,128)S(1)}, f32[2,8,256,2304]{2,3,1,0:T(8,128)}) fusion(bf16[256,2,8,128]{3,0,2,1:T(8,128)(2,1)S(1)} %bitcast.103, pred[256,2304]{0,1:T(8,128)(4,1)S(1)} %fusion.39, bf16[256,2,128]{2,0,1:T(8,128)(2,1)S(1)} %dynamic-slice_bitcast_fusion.2, bf16[2048,2,128]{2,0,1:T(8,128)(2,1)S(1)} %copy.60), kind=kOutput, calls=%fused_computation.50.clone.1 | convolution fusion | flops 2456029440 | bytes 40583168 | tf_op jit(solution)/shard_map/while/body/eval_jaxpr/sub | solution.py:85
  425.6 2.2 gather_fusion.1
  429.1 13.3 %fusion.42 = bf16[2,128,8,256]{3,1,2,0:T(8,128)(2,1)S(1)} fusion(f32[2,8,256,2304]{2,3,1,0:T(8,128)} %get-tuple-element.232, f32[2,8,256]{2,1,0:T(8,128)S(1)} %get-tuple-element.233, bf16[256,2,128]{0,2,1:T(8,128)(2,1)S(1)} %bitcast.109, bf16[2048,2,128]{0,2,1:T(8,128)(2,1)S(1)} %copy.62), kind=kOutput, calls=%fused_computation.14.clone.1 | convolution fusion | flops 2437677056 | bytes 39993344 | tf_op jit(solution)/shard_map/while/body/eval_jaxpr/kgnm,mkd->nkgd/dot_general | solution.py:87
  443.0 1.0 constant_dynamic-update-slice_fusion.2
  (57 shorter events, 10.9 us)
Async XLA Ops:
  7.2 23.3 %copy-start.1 = (f32[256,1024]{1,0:T(8,128)S(1)}, f32[256,1024]{1,0:T(8,128)}, u32[]{:S(2)}) copy-start(f32[256,1024]{1,0:T(8,128)} %param.13) | copy-start | bytes 3145732
  7.2 154.2 %all-gather.6.cloned.1.call-start = ((), (), s32[]{:S(2)}) async-start(), calls=%async_computation.4 | async-start | bytes 4718592 | tf_op jit(solution)/shard_map/all_gather | solution.py:50
  30.4 138.8 %all-gather.4.cloned.1.call-start = ((), (), s32[]{:S(2)}) async-start(), calls=%async_computation.3 | async-start | bytes 4718592 | tf_op jit(solution)/shard_map/all_gather | solution.py:51
  48.3 271.8 %all-gather.8.cloned.1.call-start = ((), (), s32[]{:S(2)}) async-start(), calls=%async_computation.5 | async-start | bytes 37748736 | tf_op jit(solution)/shard_map/all_gather | solution.py:49
  160.0 0.7 copy-start.2
  350.2 7.7 %copy-start.3 = (s32[1,2,16]{2,1,0:T(2,128)S(1)}, s32[1,2,16]{2,1,0:T(2,128)}, u32[]{:S(2)}) copy-start(s32[1,2,16]{2,1,0:T(2,128)} %param.17) | copy-start | bytes 388
  354.1 3.7 copy-start
Sparse Core Ops, SparseCore 0:
  30.5 35.6 all-gather.5
  68.7 36.5 all-gather.3
  160.2 159.7 all-gather.7
where the time goes:
time: 451 us
  waiting for transfers between devices  140 us (31%)
  blocking collectives  135 us (30%)
  matrix products  103 us (23%)
  local copies, waits for them, and re-layouts  44 us (10%)
  between operations  13.9 us (3%)
  other arithmetic  13.8 us (3%)
    all_gather x1, waiting for transfers between devices, per_device(): lax.all_gather(slabs[0], 'rep', axis=0, tiled=True)  140 us
    all_to_all x1, blocking collectives, per_device(): lax.all_to_all(weights[0], 'tp', split_axis=1, concat_axis=0, tiled=True)  97.8 us
    sub x2, matrix products, one_sequence(): expons = jnp.exp(scores - maxima)  34.9 us
    dot_general x2, matrix products, one_sequence(): jnp.einsum('kgnm,mkd->nkgd', probs, all_values, preferred_element_type=jn...  26.5 us
    reshape x1, matrix products, per_device(): raw_query.reshape(TOK, kv_local * group_size, HEAD_DIM)  25.8 us
    all_to_all x1, blocking collectives, per_device(): lax.all_to_all(weights[1], 'tp', split_axis=1, concat_axis=0, tiled=True)  20.6 us
    all_to_all x1, blocking collectives, per_device(): lax.all_to_all(weights[2], 'tp', split_axis=1, concat_axis=0, tiled=True)  16.6 us
    dot_general x2, matrix products, per_device(): jnp.dot(tokens, piece, preferred_element_type=jnp.float32)  16.1 us
  transfers between devices with their start and end apart: 3, of which 1 were waited for; matrix products, arithmetic and copies ran while one was open for 8% of the time, Pallas kernels for 0%

commit v1 on v0

v1 whole, which is shorter than its diff:
```python
import functools
import math

import jax
import jax.numpy as jnp
from jax import lax
from jax.experimental import pallas as pl
from jax.experimental.pallas import tpu as pltpu
from jax.sharding import PartitionSpec as P

HEADS = 64
KV_HEADS = 8
HEAD_DIM = 128
CHUNK_HEADS = 4
ROPE_THETA = 500000.0


def rope_tables(positions):
    half_dim = HEAD_DIM // 2
    frequency = ROPE_THETA ** (-2.0 * jnp.arange(half_dim, dtype=jnp.float32) / HEAD_DIM)
    angles = positions.astype(jnp.float32)[:, None] * frequency[None, :]
    cosine = jnp.cos(angles)
    sine = jnp.sin(angles)
    return (
        jnp.concatenate([cosine, cosine], axis=-1),
        jnp.concatenate([-sine, sine], axis=-1),
    )


def rotate(vectors, cosine, sine):
    half_dim = HEAD_DIM // 2
    swapped = jnp.concatenate([vectors[..., half_dim:], vectors[..., :half_dim]], axis=-1)
    return vectors * cosine[:, None, :] + swapped * sine[:, None, :]


def attention_kernel(*refs):
    raw_ref, cos_ref, sin_ref, old_k, old_v, new_k, new_v, bias_ref = refs[:8]
    out_ref = refs[-1]
    factor = math.log2(math.e) / math.sqrt(HEAD_DIM)
    raw = raw_ref[...]
    query = raw * cos_ref[...] + pltpu.roll(raw, HEAD_DIM // 2, 1) * sin_ref[...]
    query = query.astype(jnp.bfloat16)
    contract = (((1,), (1,)), ((), ()))
    far = lax.dot_general(query, old_k[0], contract, preferred_element_type=jnp.float32)
    far = far + bias_ref[0]
    near = lax.dot_general(query, new_k[...], contract, preferred_element_type=jnp.float32)
    row = lax.broadcasted_iota(jnp.int32, near.shape, 0)
    column = lax.broadcasted_iota(jnp.int32, near.shape, 1)
    near = jnp.where(column <= row, near, -1e30)
    top = jnp.maximum(
        jnp.max(far, axis=-1, keepdims=True), jnp.max(near, axis=-1, keepdims=True)
    )
    far = jnp.exp2((far - top) * factor)
    near = jnp.exp2((near - top) * factor)
    total = jnp.sum(far, axis=-1, keepdims=True) + jnp.sum(near, axis=-1, keepdims=True)
    result = jnp.dot(far.astype(jnp.bfloat16), old_v[0], preferred_element_type=jnp.float32)
    result += jnp.dot(near.astype(jnp.bfloat16), new_v[...], preferred_element_type=jnp.float32)
    out_ref[...] = (result / total).astype(jnp.bfloat16)


def attention(chunk, raw, cosine, sine, old_k, old_v, new_cache_k, new_cache_v, bias, held, width):
    seqs, cached, _ = old_k.shape
    tok = raw.shape[0]
    new = tok // seqs
    heads = raw.shape[1] // HEAD_DIM
    kv = chunk * CHUNK_HEADS // (HEADS // KV_HEADS)
    in_specs = [
        pl.BlockSpec((new, HEAD_DIM), lambda s, h: (s, h)),
        pl.BlockSpec((new, HEAD_DIM), lambda s, h: (s, 0)),
        pl.BlockSpec((new, HEAD_DIM), lambda s, h: (s, 0)),
        pl.BlockSpec((1, cached, HEAD_DIM), lambda s, h: (s, 0, kv)),
        pl.BlockSpec((1, cached, HEAD_DIM), lambda s, h: (s, 0, kv)),
        pl.BlockSpec((new, HEAD_DIM), lambda s, h: (s, kv)),
        pl.BlockSpec((new, HEAD_DIM), lambda s, h: (s, kv)),
        pl.BlockSpec((1, 1, cached), lambda s, h: (s, 0, 0)),
    ]
    operands = [raw, cosine, sine, old_k, old_v, new_cache_k, new_cache_v, bias]
    aliases = {}
    if held is not None:
        in_specs.append(pl.BlockSpec(memory_space=pl.ANY))
        operands.append(held)
        aliases = {8: 0}
    keys = cached + new
    return pl.pallas_call(
        attention_kernel,
        grid=(seqs, heads),
        out_shape=jax.ShapeDtypeStruct((tok, width), jnp.bfloat16),
        in_specs=in_specs,
        out_specs=pl.BlockSpec((new, HEAD_DIM), lambda s, h: (s, chunk * CHUNK_HEADS + h)),
        input_output_aliases=aliases,
        compiler_params=pltpu.CompilerParams(vmem_limit_bytes=32 * 1024 * 1024),
        cost_estimate=pl.CostEstimate(
            flops=4 * tok * heads * keys * HEAD_DIM,
            bytes_accessed=2 * 2 * seqs * keys * HEAD_DIM + 6 * tok * heads * HEAD_DIM,
            transcendentals=tok * heads * keys,
        ),
    )(*operands)


def per_device(
    tp,
    tokens,
    query_weight,
    key_weight,
    value_weight,
    cache_keys,
    cache_values,
    lengths,
    page_table,
):
    kv_local = KV_HEADS // tp
    kv_width = kv_local * HEAD_DIM
    q_width = HEADS // tp * HEAD_DIM
    chunk_width = CHUNK_HEADS * HEAD_DIM
    tok = tokens.shape[0]
    seqs, pages = page_table.shape[1:]
    new = tok // seqs
    page = cache_keys.shape[1]

    def slab(parts):
        local = jnp.stack(parts).astype(jnp.bfloat16)
        mixed = lax.all_to_all(local, "tp", split_axis=0, concat_axis=0, tiled=True)
        rows = mixed.reshape(-1, mixed.shape[-1])
        return lax.all_gather(rows, "rep", axis=0, tiled=True)

    def columns(weight, start, width, whole):
        return [weight[:, t * whole + start : t * whole + start + width] for t in range(tp)]

    slabs = [
        slab(
            [
                jnp.concatenate(pair, axis=1)
                for pair in zip(
                    columns(key_weight, 0, kv_width, kv_width),
                    columns(value_weight, 0, kv_width, kv_width),
                )
            ]
        )
    ]
    for start in range(0, q_width, chunk_width):
        slabs.append(slab(columns(query_weight, start, chunk_width, q_width)))

    seq_lengths = lengths[0]
    positions = (seq_lengths[:, None] + jnp.arange(new, dtype=jnp.int32)[None, :]).reshape(tok)
    cosine, sine = rope_tables(positions)
    order = page_table[0].reshape(-1)
    old_k = cache_keys[order].reshape(seqs, pages * page, kv_width)
    old_v = cache_values[order].reshape(seqs, pages * page, kv_width)
    visible = jnp.arange(pages * page, dtype=jnp.int32)[None, :] < seq_lengths[:, None]
    bias = jnp.where(visible, 0.0, -1e30).astype(jnp.float32)[:, None, :]

    raw_kv = jnp.dot(tokens, slabs[0], preferred_element_type=jnp.float32)
    new_k = rotate(raw_kv[:, :kv_width].reshape(tok, kv_local, HEAD_DIM), cosine, sine)
    new_k = new_k.astype(jnp.bfloat16).reshape(tok, kv_width)
    new_v = raw_kv[:, kv_width:].astype(jnp.bfloat16)

    attended = None
    for chunk, piece in enumerate(slabs[1:]):
        raw = jnp.dot(tokens, piece, preferred_element_type=jnp.float32)
        attended = attention(
            chunk, raw, cosine, sine, old_k, old_v, new_k, new_v, bias, attended, q_width
        )
    return attended, jnp.stack([new_k, new_v])


def solution(mesh):
    return jax.shard_map(
        functools.partial(per_device, mesh.shape["tp"]),
        mesh=mesh,
        in_specs=(
            P("rep", None),
            P(("rep", "tp"), None),
            P(("rep", "tp"), None),
            P(("rep", "tp"), None),
            P("rep", None, "tp"),
            P("rep", None, "tp"),
            P("rep", None),
            P("rep", None, None),
        ),
        out_specs=(P("rep", "tp"), P(None, "rep", "tp")),
        check_vma=False,
    )
```

time: 451 us -> 350 us (0.78)
  waiting for transfers between devices: 140 us -> 72 us
  matrix products: 103 us -> 48.8 us
  Pallas kernels: 0 us -> 48.3 us
  local copies, waits for them, and re-layouts: 44 us -> 9.32 us
  blocking collectives: 135 us -> 144 us
    all_gather x3 -> x5, waiting for transfers between devices: 140 us -> 71.9 us  [slab(): return lax.all_gather(rows, 'rep', axis=0, tiled=True)]
    pallas_call x0 -> x4, Pallas kernels: none -> 48.3 us  [attention(): pl.pallas_call(attention_kernel, grid=(seqs, heads), out_shape=jax.ShapeD...]
    sub x2 -> x0, matrix products: 34.9 us -> none  [one_sequence(): expons = jnp.exp(scores - maxima)]
    reshape x1 -> x0, matrix products: 25.8 us -> none  [per_device(): raw_query.reshape(TOK, kv_local * group_size, HEAD_DIM)]
    unnamed x12 -> x23, local copies, waits for them, and re-layouts: 9.93 us -> 0.06 us
    all_to_all x3 -> x5, blocking collectives: 135 us -> 144 us  [slab(): mixed = lax.all_to_all(local, 'tp', split_axis=0, concat_axis=0, tiled=True)]
    all_to_all x3 -> x0, local copies, waits for them, and re-layouts: 8.28 us -> none  [the longest x1 6.28 us: per_device(): lax.all_to_all(weights[0], 'tp', split_axis=1, concat_axis=0, tiled=True)]
    another operation x3 -> x11, other arithmetic: 3.86 us -> 10.6 us
  transfers between devices with their start and end apart: 3 -> 5, of which waited for: 1 -> 3; matrix products, arithmetic and copies ran while one was open for 8% -> 16% of each run, Pallas kernels for 0% -> 10%
where the time goes in v1:
time: 350 us; the launch traced here: 349 us
  blocking collectives  144 us (41%)
  waiting for transfers between devices  72 us (21%)
  matrix products  48.8 us (14%)
  Pallas kernels  48.3 us (14%)
  between operations  14.1 us (4%)
  other arithmetic  12.8 us (4%)
  local copies, waits for them, and re-layouts  9.32 us (3%)
    all_to_all x5, blocking collectives, slab(): mixed = lax.all_to_all(local, 'tp', split_axis=0, concat_axis=0, tiled=True)  144 us
    all_gather x5, waiting for transfers between devices, slab(): return lax.all_gather(rows, 'rep', axis=0, tiled=True)  71.9 us
    pallas_call x4, Pallas kernels, attention(): pl.pallas_call(attention_kernel, grid=(seqs, heads), out_shape=jax.ShapeD...  48.3 us
    dot_general x4, matrix products, per_device(): raw = jnp.dot(tokens, piece, preferred_element_type=jnp.float32)  39.3 us
    dot_general x1, matrix products, per_device(): raw_kv = jnp.dot(tokens, slabs[0], preferred_element_type=jnp.float32)  9.46 us
  transfers between devices with their start and end apart: 5, of which 3 were waited for; matrix products, arithmetic and copies ran while one was open for 16% of the time, Pallas kernels for 10%

profile of v1, /device:TPU:0, one launch (start us, length us, event | category | flops | bytes accessed | tf_op | source)
XLA Modules:
  0.0 349.3 jit_solution(1167992547190336666)
XLA Ops:
  7.2 1.4 convert.83
  8.7 1.3 convert.82
  10.3 32.0 %all_to_all.25 = bf16[4,256,512]{2,1,0:T(8,128)(2,1)} all-to-all(bf16[4,256,512]{2,1,0:T(8,128)(2,1)S(1)} %pad_maximum_fusion.1), channel_id=1, replica_groups=mesh['rep'=8,'tp'=4] {'tp'}, dimensions={0} | all-to-all | bytes 2097152 | tf_op jit(solution)/shard_map/all_to_all | solution.py:122
  42.3 3.9 %convert.81 = bf16[256,8192]{1,0:T(8,128)(2,1)S(1)} convert(f32[256,8192]{1,0:T(8,128)} %param.9) | non-fusion elementwise | flops 2097152 | bytes 12582912 | tf_op jit(solution)/shard_map/convert.72
  46.3 1.3 slice_bitcast_fusion.3
  47.7 28.1 %all_to_all.26 = bf16[4,256,512]{2,1,0:T(8,128)(2,1)} all-to-all(bf16[4,256,512]{2,1,0:T(8,128)(2,1)S(1)} %pad_maximum_fusion.4), channel_id=1, replica_groups=mesh['rep'=8,'tp'=4] {'tp'}, dimensions={0} | all-to-all | bytes 2097152 | tf_op jit(solution)/shard_map/all_to_all | solution.py:122
  75.8 1.3 pad_maximum_fusion.3
  77.2 27.9 %all_to_all.27 = bf16[4,256,512]{2,1,0:T(8,128)(2,1)} all-to-all(bf16[4,256,512]{2,1,0:T(8,128)(2,1)S(1)} %pad_maximum_fusion.3), channel_id=1, replica_groups=mesh['rep'=8,'tp'=4] {'tp'}, dimensions={0} | all-to-all | bytes 2097152 | tf_op jit(solution)/shard_map/all_to_all | solution.py:122
  105.1 1.3 pad_maximum_fusion.2
  106.5 28.0 %all_to_all.28 = bf16[4,256,512]{2,1,0:T(8,128)(2,1)} all-to-all(bf16[4,256,512]{2,1,0:T(8,128)(2,1)S(1)} %pad_maximum_fusion.2), channel_id=1, replica_groups=mesh['rep'=8,'tp'=4] {'tp'}, dimensions={0} | all-to-all | bytes 2097152 | tf_op jit(solution)/shard_map/all_to_all | solution.py:122
  134.6 27.9 %all_to_all.29 = bf16[4,256,512]{2,1,0:T(8,128)(2,1)} all-to-all(bf16[4,256,512]{2,1,0:T(8,128)(2,1)S(1)} %pad_maximum_fusion), channel_id=1, replica_groups=mesh['rep'=8,'tp'=4] {'tp'}, dimensions={0} | all-to-all | bytes 2097152 | tf_op jit(solution)/shard_map/all_to_all | solution.py:122
  162.8 2.0 gather_fusion
  164.8 3.6 %gather_fusion.1 = bf16[32,128,256]{2,1,0:T(8,128)(2,1)} fusion(bf16[32,128,256]{2,1,0:T(8,128)(2,1)} %param.13, s32[1024]{0:T(1024)S(1)} %pad_clamp_fusion), kind=kCustom, calls=%fused_computation.1 | custom fusion | bytes 4194432 | tf_op jit(solution)/shard_map/gather | solution.py:148
  168.4 1.0 fusion.1
  169.4 0.2 pad_maximum_fusion.6
  169.7 9.5 %convolution_bitcast_fusion.3 = f32[512,512]{1,0:T(8,128)S(1)} fusion(bf16[512,8192]{1,0:T(8,128)(2,1)} %param.8, bf16[8192,512]{1,0:T(8,128)(2,1)} %all-gather.8.cloned.1.call-done), kind=kOutput, calls=%fused_computation.5 | convolution fusion | flops 4294967296 | bytes 17825792 | tf_op jit(solution)/shard_map/dot_general | solution.py:152
  179.3 0.3 reshape.143
  179.6 0.6 fusion.3
  180.2 0.6 maximum_multiply_fusion
  181.2 10.6 %convolution_bitcast_fusion.refs_0_ = f32[512,512]{1,0:T(8,128)S(1)} fusion(bf16[512,8192]{1,0:T(8,128)(2,1)} %param.8, bf16[8192,512]{1,0:T(8,128)(2,1)} %all-gather.14.cloned.1.call-done), kind=kOutput, calls=%fused_computation.2 | convolution fusion | flops 4294967296 | bytes 17825792 | tf_op jit(solution)/shard_map/dot_general | solution.py:159
  191.8 12.0 %shard_map.95.refs_8_ = bf16[512,2048]{1,0:T(8,128)(2,1)} custom-call(f32[512,512]{1,0:T(8,128)S(1)} %convolution_bitcast_fusion.refs_0_, f32[512,128]{1,0:T(8,128)S(1)} %get-tuple-element.31.refs_1_, f32[512,128]{1,0:T(8,128)S(1)} %get-tuple-element.32.refs_2_, bf16[2,2048,256]{2,1,0:T(8,128)(2,1)S(1)} %bitcast.86, bf16[2,2048,256]{2,1,0:T(8,128)(2,1)S(1)} %bitcast.90, ...), custom_call_target="tpu_custom_call" | custom-call | flops 2415919104 | bytes 3932160 | tf_op jit(solution)/shard_map/pallas_call | solution.py:84
  203.8 4.4 %all-gather.12.cloned.1.call-done = bf16[8192,512]{1,0:T(8,128)(2,1)} async-done(((bf16[1024,512]{1,0:T(8,128)(2,1)}), bf16[8192,512]{1,0:T(8,128)(2,1)}) %all-gather.12.cloned.1.call-update) | async-done | bytes 8388624 | tf_op jit(solution)/shard_map/all_gather | solution.py:124
  208.2 9.6 %convolution_bitcast_fusion.1.refs_0_ = f32[512,512]{1,0:T(8,128)S(1)} fusion(bf16[512,8192]{1,0:T(8,128)(2,1)} %param.8, bf16[8192,512]{1,0:T(8,128)(2,1)} %all-gather.12.cloned.1.call-done), kind=kOutput, calls=%fused_computation.3 | convolution fusion | flops 4294967296 | bytes 17825792 | tf_op jit(solution)/shard_map/dot_general | solution.py:159
  217.8 12.3 %shard_map.96.refs_8_ = bf16[512,2048]{1,0:T(8,128)(2,1)} custom-call(f32[512,512]{1,0:T(8,128)S(1)} %convolution_bitcast_fusion.1.refs_0_, f32[512,128]{1,0:T(8,128)S(1)} %get-tuple-element.31.refs_1_, f32[512,128]{1,0:T(8,128)S(1)} %get-tuple-element.32.refs_2_, bf16[2,2048,256]{2,1,0:T(8,128)(2,1)S(1)} %bitcast.87, ...), custom_call_target="tpu_custom_call", output_to_operand_aliasing={{}: (8, {})} | custom-call | flops 2415919104 | bytes 3932160 | tf_op jit(solution)/shard_map/pallas_call | solution.py:84
  230.0 34.2 %all-gather.10.cloned.1.call-done = bf16[8192,512]{1,0:T(8,128)(2,1)} async-done(((bf16[1024,512]{1,0:T(8,128)(2,1)}), bf16[8192,512]{1,0:T(8,128)(2,1)}) %all-gather.10.cloned.1.call-update) | async-done | bytes 8388624 | tf_op jit(solution)/shard_map/all_gather | solution.py:124
  264.2 9.6 %convolution_bitcast_fusion.2.refs_0_ = f32[512,512]{1,0:T(8,128)S(1)} fusion(bf16[512,8192]{1,0:T(8,128)(2,1)} %param.8, bf16[8192,512]{1,0:T(8,128)(2,1)} %all-gather.10.cloned.1.call-done), kind=kOutput, calls=%fused_computation.4 | convolution fusion | flops 4294967296 | bytes 17825792 | tf_op jit(solution)/shard_map/dot_general | solution.py:159
  273.8 12.0 %shard_map.97.refs_8_ = bf16[512,2048]{1,0:T(8,128)(2,1)} custom-call(f32[512,512]{1,0:T(8,128)S(1)} %convolution_bitcast_fusion.2.refs_0_, f32[512,128]{1,0:T(8,128)S(1)} %get-tuple-element.31.refs_1_, f32[512,128]{1,0:T(8,128)S(1)} %get-tuple-element.32.refs_2_, bf16[2,2048,256]{2,1,0:T(8,128)(2,1)S(1)} %bitcast.88, ...), custom_call_target="tpu_custom_call", output_to_operand_aliasing={{}: (8, {})} | custom-call | flops 2415919104 | bytes 3932160 | tf_op jit(solution)/shard_map/pallas_call | solution.py:84
  285.8 1.1 slice_bitcast_fusion.16
  286.9 33.3 %all-gather.6.cloned.1.call-done = bf16[8192,512]{1,0:T(8,128)(2,1)} async-done(((bf16[1024,512]{1,0:T(8,128)(2,1)}), bf16[8192,512]{1,0:T(8,128)(2,1)}) %all-gather.6.cloned.1.call-update) | async-done | bytes 8388624 | tf_op jit(solution)/shard_map/all_gather | solution.py:124
  320.2 9.6 %convolution_bitcast_fusion.4.refs_0_ = f32[512,512]{1,0:T(8,128)S(1)} fusion(bf16[512,8192]{1,0:T(8,128)(2,1)} %param.8, bf16[8192,512]{1,0:T(8,128)(2,1)} %all-gather.6.cloned.1.call-done), kind=kOutput, calls=%fused_computation.6 | convolution fusion | flops 4294967296 | bytes 17825792 | tf_op jit(solution)/shard_map/dot_general | solution.py:159
  329.8 12.0 %shard_map.98 = bf16[512,2048]{1,0:T(8,128)(2,1)} custom-call(f32[512,512]{1,0:T(8,128)S(1)} %convolution_bitcast_fusion.4.refs_0_, f32[512,128]{1,0:T(8,128)S(1)} %get-tuple-element.31.refs_1_, f32[512,128]{1,0:T(8,128)S(1)} %get-tuple-element.32.refs_2_, bf16[2,2048,256]{2,1,0:T(8,128)(2,1)S(1)} %bitcast.89, ...), custom_call_target="tpu_custom_call", output_to_operand_aliasing={{}: (8, {})} | custom-call | flops 2415919104 | bytes 3932160 | tf_op jit(solution)/shard_map/pallas_call | solution.py:84
  341.9 0.8 pad_maximum_fusion.5
  (52 shorter events, 1.6 us)
Async XLA Ops:
  7.2 155.6 %copy-start = (bf16[32,128,256]{2,1,0:T(8,128)(2,1)S(1)}, bf16[32,128,256]{2,1,0:T(8,128)(2,1)}, u32[]{:S(2)}) copy-start(bf16[32,128,256]{2,1,0:T(8,128)(2,1)} %param.12) | copy-start | bytes 6291460
  7.2 162.5 %all-gather.8.cloned.1.call-start = ((), (), s32[]{:S(2)}) async-start(), calls=%async_computation.6 | async-start | bytes 9437184 | tf_op jit(solution)/shard_map/all_gather | solution.py:124
  42.3 138.9 %all-gather.14.cloned.1.call-start = ((), (), s32[]{:S(2)}) async-start(), calls=%async_computation.9 | async-start | bytes 9437184 | tf_op jit(solution)/shard_map/all_gather | solution.py:124
  75.8 86.8 %copy-start.9 = (s32[1,2]{1,0:T(1,128)S(1)}, s32[1,2]{1,0:T(1,128)}, u32[]{:S(2)}) copy-start(s32[1,2]{1,0:T(1,128)} %param.14) | copy-start | bytes 28
  75.8 86.9 %copy-start.10 = (s32[1,2,16]{2,1,0:T(2,128)S(1)}, s32[1,2,16]{2,1,0:T(2,128)}, u32[]{:S(2)}) copy-start(s32[1,2,16]{2,1,0:T(2,128)} %param.15) | copy-start | bytes 388
  75.8 132.4 %all-gather.12.cloned.1.call-start = ((), (), s32[]{:S(2)}) async-start(), calls=%async_computation.8 | async-start | bytes 9437184 | tf_op jit(solution)/shard_map/all_gather | solution.py:124
  105.1 159.1 %all-gather.10.cloned.1.call-start = ((), (), s32[]{:S(2)}) async-start(), calls=%async_computation.7 | async-start | bytes 9437184 | tf_op jit(solution)/shard_map/all_gather | solution.py:124
  134.4 185.8 %all-gather.6.cloned.1.call-start = ((), (), s32[]{:S(2)}) async-start(), calls=%async_computation.5 | async-start | bytes 9437184 | tf_op jit(solution)/shard_map/all_gather | solution.py:124
  179.2 1.8 copy-start.8
  181.2 10.6 %copy-start.2 = (bf16[32,128,256]{2,1,0:T(8,128)(2,1)S(1)}, bf16[32,128,256]{2,1,0:T(8,128)(2,1)}, u32[]{:S(2)}) copy-start(bf16[32,128,256]{2,1,0:T(8,128)(2,1)} %gather_fusion) | copy-start | bytes 6291460
  181.2 10.6 %copy-start.4 = (bf16[32,128,256]{2,1,0:T(8,128)(2,1)S(1)}, bf16[32,128,256]{2,1,0:T(8,128)(2,1)}, u32[]{:S(2)}) copy-start(bf16[32,128,256]{2,1,0:T(8,128)(2,1)} %gather_fusion.1) | copy-start | bytes 6291460
  208.2 9.6 %copy-start.5 = (bf16[32,128,256]{2,1,0:T(8,128)(2,1)S(1)}, bf16[32,128,256]{2,1,0:T(8,128)(2,1)}, u32[]{:S(2)}) copy-start(bf16[32,128,256]{2,1,0:T(8,128)(2,1)} %gather_fusion.1) | copy-start | bytes 6291460
  264.2 9.6 %copy-start.6 = (bf16[32,128,256]{2,1,0:T(8,128)(2,1)S(1)}, bf16[32,128,256]{2,1,0:T(8,128)(2,1)}, u32[]{:S(2)}) copy-start(bf16[32,128,256]{2,1,0:T(8,128)(2,1)} %gather_fusion.1) | copy-start | bytes 6291460
  320.2 9.6 %copy-start.3 = (bf16[32,128,256]{2,1,0:T(8,128)(2,1)S(1)}, bf16[32,128,256]{2,1,0:T(8,128)(2,1)}, u32[]{:S(2)}) copy-start(bf16[32,128,256]{2,1,0:T(8,128)(2,1)} %gather_fusion) | copy-start | bytes 6291460
  320.2 9.6 %copy-start.7 = (bf16[32,128,256]{2,1,0:T(8,128)(2,1)S(1)}, bf16[32,128,256]{2,1,0:T(8,128)(2,1)}, u32[]{:S(2)}) copy-start(bf16[32,128,256]{2,1,0:T(8,128)(2,1)} %gather_fusion.1) | copy-start | bytes 6291460
  320.2 22.5 %copy-start.1 = (bf16[32,128,256]{2,1,0:T(8,128)(2,1)S(1)}, bf16[32,128,256]{2,1,0:T(8,128)(2,1)}, u32[]{:S(2)}) copy-start(bf16[32,128,256]{2,1,0:T(8,128)(2,1)} %param.12) | copy-start | bytes 6291460
Sparse Core Ops, SparseCore 0:
  42.4 53.3 all-gather.7
  97.7 54.2 all-gather.13
  153.9 54.2 all-gather.11
  209.9 54.2 all-gather.9
  265.9 54.2 all-gather.5
